TPU v7x, 32 devices: a whole 2x2x4 slice. The times are simulated.
32 devices in a mesh: gx: 8 (over y, x, core), gy: 4 (over z).
Axes of the slice: x: 2, y: 2, z: 4, core: 2. Of those that a mesh axis runs over, the one named last changes fastest.
Arguments:
- rhs_conc: float32 [16, 64, 2048], P('gx', 'gy'), may hold values from -60 to 60
- rhs_pots: float32 [16, 64, 33], P('gx', 'gy'), may hold values from -60 to 60
- diffusion: float32 [16, 64, 32], P('gx', 'gy'), may hold values from 0.05 to 5
- exchange: float32 [16, 64, 32], P('gx', 'gy'), may hold values from 0.2 to 4
- slope: float32 [16, 64, 32], P('gx', 'gy'), may hold values from 0.1 to 1
Outputs:
- sol_conc: float32 [16, 64, 2048], P('gx', 'gy')
- sol_pots: float32 [16, 64, 33], P('gx', 'gy')
All inputs are finite; a program needn't handle non-finite values.
Results may differ from a plain program's by a relative error of at most 0.0003.
Values sent between devices are 32-bit elements; how exact they have to be, the bound alone decides.
A program may use at most 64 MiB of HBM per device.

v0:
```python
import jax
import jax.numpy as jnp
from jax import lax
from jax.sharding import PartitionSpec as P

ITERS = 10


node_cond = 1.0
plane_cond = 0.5
collector_cond = 2.0
epsilon = 1e-06


def padded_2(cells, sides, width):
    for axis, dim in sides:
        count = lax.axis_size(axis)
        ends = count - 1
        head = lax.slice_in_dim(cells, 0, width, axis=dim)
        tail = lax.slice_in_dim(cells, cells.shape[dim] - width, cells.shape[dim], axis=dim)
        cells = jnp.concatenate(
            [
                lax.ppermute(tail, axis, [(i, (i + 1) % count) for i in range(ends)]),
                cells,
                lax.ppermute(head, axis, [((i + 1) % count, i) for i in range(ends)]),
            ],
            axis=dim,
        )
    return cells


def mirror_laplace(values):
    inner = jnp.concatenate([values[..., :1], values[..., :-1]], axis=-1)
    outer = jnp.concatenate([values[..., 1:], values[..., -1:]], axis=-1)
    return 2.0 * values - inner - outer


def local_operator(conc, padded, diffusion, exchange, slope):
    nodes = exchange.shape[2]
    shell_count = conc.shape[2] // nodes
    shells = conc.reshape(conc.shape[0], conc.shape[1], nodes, shell_count)
    center = padded[1:-1, 1:-1]
    lateral = (
        4.0 * center - padded[2:, 1:-1] - padded[:-2, 1:-1] - padded[1:-1, 2:] - padded[1:-1, :-2]
    )
    node_pot = center[..., :nodes]
    collector = center[..., nodes]
    current = exchange * (node_pot - collector[..., None])
    surface = shells[..., shell_count - 1]
    surface_flag = (lax.broadcasted_iota(jnp.int32, (shell_count,), 0) == shell_count - 1).astype(
        jnp.float32
    )
    new_shells = (
        shells + diffusion[..., None] * mirror_laplace(shells) + current[..., None] * surface_flag
    )
    new_nodes = (
        node_cond * mirror_laplace(node_pot)
        + current
        - slope * surface
        + plane_cond * lateral[..., :nodes]
    )
    new_collector = collector_cond * lateral[..., nodes] - jnp.mean(current, axis=-1)
    return (
        new_shells.reshape(conc.shape),
        jnp.concatenate([new_nodes, new_collector[..., None]], axis=-1),
    )


def least_squares(columns, start_norm):
    count = len(columns)
    target = [start_norm] + [jnp.zeros_like(start_norm) for step in range(count)]
    cosines = []
    sines = []
    upper_rows = []
    for step in range(count):
        entries = list(columns[step])
        for row in range(step):
            first = cosines[row] * entries[row] + sines[row] * entries[row + 1]
            second = cosines[row] * entries[row + 1] - sines[row] * entries[row]
            entries[row] = first
            entries[row + 1] = second
        radius = jnp.sqrt(entries[step] * entries[step] + entries[step + 1] * entries[step + 1])
        cosine = entries[step] / radius
        sine = entries[step + 1] / radius
        entries[step] = radius
        cosines.append(cosine)
        sines.append(sine)
        lead = target[step]
        target[step] = cosine * lead
        target[step + 1] = -sine * lead
        upper_rows.append(entries[: step + 1])
    weights = [None] * count
    for row in range(count - 1, -1, -1):
        total = target[row]
        for later in range(row + 1, count):
            total = total - upper_rows[later][row] * weights[later]
        weights[row] = total / upper_rows[row][row]
    return weights


def shards(rhs_conc, rhs_pots, diffusion, exchange, slope):
    local_square = jnp.sum(rhs_conc * rhs_conc) + jnp.sum(rhs_pots * rhs_pots)
    start_norm = jnp.sqrt(lax.psum(local_square, ("gx", "gy")) + epsilon)
    basis = [(rhs_conc / start_norm, rhs_pots / start_norm)]
    columns = []
    for step in range(ITERS):
        padded = padded_2(basis[step][1], (("gx", 0), ("gy", 1)), 1)
        image_conc, image_pots = local_operator(basis[step][0], padded, diffusion, exchange, slope)
        local_dots = jnp.stack(
            [jnp.sum(vector[0] * image_conc) + jnp.sum(vector[1] * image_pots) for vector in basis]
        )
        image_square = jnp.sum(image_conc * image_conc) + jnp.sum(image_pots * image_pots)
        coeffs, total_square = lax.psum((local_dots, image_square), ("gx", "gy"))
        rest_conc, rest_pots = (image_conc, image_pots)
        for row in range(step + 1):
            rest_conc = rest_conc - coeffs[row] * basis[row][0]
            rest_pots = rest_pots - coeffs[row] * basis[row][1]
        height = jnp.sqrt(total_square - jnp.sum(coeffs * coeffs) + epsilon)
        basis.append((rest_conc / height, rest_pots / height))
        columns.append([coeffs[row] for row in range(step + 1)] + [height])
    weights = least_squares(columns, start_norm)
    sol_conc = weights[0] * basis[0][0]
    sol_pots = weights[0] * basis[0][1]
    for step in range(1, ITERS):
        sol_conc = sol_conc + weights[step] * basis[step][0]
        sol_pots = sol_pots + weights[step] * basis[step][1]
    return (sol_conc, sol_pots)


def solution(mesh):
    return jax.shard_map(
        shards,
        mesh=mesh,
        in_specs=(
            P("gx", "gy", None),
            P("gx", "gy", None),
            P("gx", "gy", None),
            P("gx", "gy", None),
            P("gx", "gy", None),
        ),
        out_specs=(P("gx", "gy", None), P("gx", "gy", None)),
        check_vma=False,
    )
```

profile of v0, /device:TPU:0, one launch (start us, length us, event | category | flops | bytes accessed | tf_op | source)
XLA Modules:
  0.0 950.6 jit_solution(5201951569017878183)
XLA Ops:
  2.0 1.7 multiply_reduce_fusion.65
  5.1 42.0 %psum.147 = f32[]{:T(128)} all-reduce(f32[]{:T(128)S(6)} %add.632), channel_id=1, replica_groups=mesh['gx'=8,'gy'=4] {'gx','gy'}, use_global_device_ids=true, to_apply=%region_2.0 | all-reduce | flops 1 | bytes 8 | tf_op jit(solution)/shard_map/psum | solution.py:103
  49.2 3.0 collective-permute-start.1
  57.7 4.5 collective-permute-start.3
  62.7 1.5 collective-permute-done.3
  69.2 42.0 %all-reduce.9 = (f32[]{:T(128)}, f32[1]{0:T(128)}) all-reduce(f32[]{:T(128)S(6)} %add.639, f32[1]{0:T(128)} %bitcast.3), channel_id=1, replica_groups=mesh['gx'=8,'gy'=4] {'gx','gy'}, use_global_device_ids=true, to_apply=%region_9.0 | all-reduce | flops 2 | bytes 16 | tf_op jit(solution)/shard_map/psum | solution.py:113
  116.6 3.0 collective-permute-start.5
  124.6 4.5 collective-permute-start.7
  129.5 1.5 collective-permute-done.7
  137.5 42.3 %all-reduce.8 = (f32[]{:T(128)}, f32[2]{0:T(128)S(1)}) all-reduce(f32[]{:T(128)S(6)} %add.649, f32[2]{0:T(128)S(1)} %pad_maximum_fusion.120), channel_id=1, replica_groups=mesh['gx'=8,'gy'=4] {'gx','gy'}, use_global_device_ids=true, to_apply=%region_18.0 | all-reduce | flops 3 | bytes 24 | tf_op jit(solution)/shard_map/psum | solution.py:113
  187.5 3.0 collective-permute-start.9
  196.1 4.7 collective-permute-start.11
  210.8 41.6 %all-reduce.7 = (f32[]{:T(128)}, f32[3]{0:T(128)S(1)}) all-reduce(f32[]{:T(128)S(6)} %add.660, f32[3]{0:T(128)S(1)} %pad_maximum_fusion.121), channel_id=1, replica_groups=mesh['gx'=8,'gy'=4] {'gx','gy'}, use_global_device_ids=true, to_apply=%region_30.0 | all-reduce | flops 4 | bytes 32 | tf_op jit(solution)/shard_map/psum | solution.py:113
  255.0 1.9 subtract_divide_fusion.15
  258.1 1.9 subtract_divide_fusion.6
  262.0 3.0 collective-permute-start.13
  271.7 4.5 collective-permute-start.15
  287.7 41.9 %all-reduce.6 = (f32[]{:T(128)}, f32[4]{0:T(128)S(1)}) all-reduce(f32[]{:T(128)S(6)} %add.672, f32[4]{0:T(128)S(1)} %pad_maximum_fusion.122), channel_id=1, replica_groups=mesh['gx'=8,'gy'=4] {'gx','gy'}, use_global_device_ids=true, to_apply=%region_44.0 | all-reduce | flops 5 | bytes 40 | tf_op jit(solution)/shard_map/psum | solution.py:113
  332.2 2.6 subtract_divide_fusion.14
  336.7 2.7 subtract_divide_fusion.5
  341.3 3.0 collective-permute-start.17
  353.1 4.5 collective-permute-start.19
  358.1 1.5 collective-permute-done.19
  370.5 41.6 %all-reduce.5 = (f32[]{:T(128)}, f32[5]{0:T(128)S(1)}) all-reduce(f32[]{:T(128)S(6)} %add.685, f32[5]{0:T(128)S(1)} %stack.210), channel_id=1, replica_groups=mesh['gx'=8,'gy'=4] {'gx','gy'}, use_global_device_ids=true, to_apply=%region_60.0 | all-reduce | flops 6 | bytes 48 | tf_op jit(solution)/shard_map/psum | solution.py:113
  414.7 3.2 subtract_divide_fusion.13
  419.1 3.2 subtract_divide_fusion.4
  424.3 3.2 collective-permute-start.21
  438.2 4.5 collective-permute-start.23
  456.9 41.9 %all-reduce.4 = (f32[]{:T(128)}, f32[6]{0:T(128)S(1)}) all-reduce(f32[]{:T(128)S(6)} %add.699, f32[6]{0:T(128)S(1)} %stack.217), channel_id=1, replica_groups=mesh['gx'=8,'gy'=4] {'gx','gy'}, use_global_device_ids=true, to_apply=%region_78.0 | all-reduce | flops 7 | bytes 56 | tf_op jit(solution)/shard_map/psum | solution.py:113
  501.4 3.7 subtract_divide_fusion.12
  506.9 3.8 subtract_divide_fusion.3
  515.4 3.0 collective-permute-start.25
  530.8 4.5 collective-permute-start.27
  539.8 1.7 multiply_reduce_fusion.31
  551.5 41.6 %all-reduce.3 = (f32[]{:T(128)}, f32[7]{0:T(128)S(1)}) all-reduce(f32[]{:T(128)S(6)} %add.714, f32[7]{0:T(128)S(1)} %stack.225), channel_id=1, replica_groups=mesh['gx'=8,'gy'=4] {'gx','gy'}, use_global_device_ids=true, to_apply=%region_98.0 | all-reduce | flops 8 | bytes 64 | tf_op jit(solution)/shard_map/psum | solution.py:113
  595.8 4.4 subtract_divide_fusion.11
  602.2 4.5 subtract_divide_fusion.2
  611.8 2.1 copy.529
  615.2 3.6 collective-permute-start.29
  618.8 2.1 pad_maximum_fusion.15
  632.6 4.8 collective-permute-start.31
  645.6 2.6 multiply_reduce_fusion.22
  659.6 40.8 %all-reduce.2 = (f32[]{:T(128)}, f32[8]{0:T(128)S(1)}) all-reduce(f32[]{:T(128)S(6)} %add.730, f32[8]{0:T(128)S(1)} %stack.234), channel_id=1, replica_groups=mesh['gx'=8,'gy'=4] {'gx','gy'}, use_global_device_ids=true, to_apply=%region_120.0 | all-reduce | flops 9 | bytes 72 | tf_op jit(solution)/shard_map/psum | solution.py:113
  703.1 5.0 subtract_divide_fusion.10
  710.7 5.1 subtract_divide_fusion.1
  723.4 2.1 copy.530
  726.8 3.6 collective-permute-start.33
  730.4 2.1 pad_maximum_fusion.17
  738.6 1.9 concatenate.447
  743.7 4.5 collective-permute-start.35
  755.7 1.7 multiply_reduce_fusion.78
  757.3 2.1 multiply_reduce_fusion.12
  772.0 41.0 %all-reduce.1 = (f32[]{:T(128)}, f32[9]{0:T(128)S(1)}) all-reduce(f32[]{:T(128)S(6)} %add.747, f32[9]{0:T(128)S(1)} %stack.244), channel_id=1, replica_groups=mesh['gx'=8,'gy'=4] {'gx','gy'}, use_global_device_ids=true, to_apply=%region_144.0 | all-reduce | flops 10 | bytes 80 | tf_op jit(solution)/shard_map/psum | solution.py:113
  815.7 5.7 subtract_divide_fusion.9
  824.0 6.6 subtract_divide_fusion
  839.7 2.1 copy.531
  843.1 3.6 collective-permute-start.37
  846.8 2.0 pad_maximum_fusion.19
  856.9 1.9 concatenate.461
  861.6 4.5 collective-permute-start.39
  872.2 2.0 mul.2912
  874.2 1.7 multiply_reduce_fusion.66
  875.9 2.1 multiply_reduce_fusion
  891.7 40.8 %all-reduce = (f32[10]{0:T(128)S(1)}, f32[]{:T(128)}) all-reduce(f32[10]{0:T(128)S(1)} %stack.255, f32[]{:T(128)S(6)} %add.765), channel_id=1, replica_groups=mesh['gx'=8,'gy'=4] {'gx','gy'}, use_global_device_ids=true, to_apply=%region_167.0 | all-reduce | flops 11 | bytes 88 | tf_op jit(solution)/shard_map/psum | solution.py:113
  (492 shorter events, 152.6 us)
Async XLA Ops:
  0.6 4.4 copy-start.43
  2.0 50.2 %copy-start = (f32[2,16,2048]{2,1,0:T(8,128)S(1)}, f32[2,16,2048]{2,1,0:T(8,128)}, u32[]{:S(2)}) copy-start(f32[2,16,2048]{2,1,0:T(8,128)} %param.5) | copy-start | bytes 786436
  47.9 8.4 collective-permute-start
  49.2 7.1 collective-permute-start.1
  56.4 6.2 collective-permute-start.2
  57.7 6.5 collective-permute-start.3
  115.3 7.8 collective-permute-start.4
  116.6 6.5 collective-permute-start.5
  123.3 6.2 collective-permute-start.6
  124.6 6.5 collective-permute-start.7
  186.2 8.4 collective-permute-start.8
  187.5 7.1 collective-permute-start.9
  194.8 6.4 collective-permute-start.10
  196.1 6.5 collective-permute-start.11
  260.7 9.5 collective-permute-start.12
  262.0 8.2 collective-permute-start.13
  270.4 6.2 collective-permute-start.14
  271.7 6.5 collective-permute-start.15
  340.0 11.7 %collective-permute-start.16 = (f32[1,16,33]{1,0,2:T(1,128)}, f32[1,16,33]{1,0,2:T(1,128)S(1)}, u32[]{:S(2)}, u32[]{:S(2)}) collective-permute-start(f32[1,16,33]{1,0,2:T(1,128)} %get-tuple-element.304), channel_id=1, source_target_pairs={{4,0},{8,4},{12,8},{16,12},{20,16},{24,20},{28,24},{5,1},{9,5},{13... | collective-permute-start | bytes 6344 | tf_op jit(solution)/shard_map/ppermute | solution.py:25
  341.3 10.4 %collective-permute-start.17 = (f32[1,16,33]{1,0,2:T(1,128)}, f32[1,16,33]{1,0,2:T(1,128)S(1)}, u32[]{:S(2)}, u32[]{:S(2)}) collective-permute-start(f32[1,16,33]{1,0,2:T(1,128)} %get-tuple-element.303), channel_id=1, source_target_pairs={{0,4},{4,8},{8,12},{12,16},{16,20},{20,24},{24,28},{1,5},{5,9},{9,... | collective-permute-start | bytes 6344 | tf_op jit(solution)/shard_map/ppermute | solution.py:23
  351.8 6.2 collective-permute-start.18
  353.1 6.5 collective-permute-start.19
  423.0 13.7 %collective-permute-start.20 = (f32[1,16,33]{1,0,2:T(1,128)S(1)}, f32[1,16,33]{1,0,2:T(1,128)S(1)}, u32[]{:S(2)}, u32[]{:S(2)}) collective-permute-start(f32[1,16,33]{1,0,2:T(1,128)S(1)} %get-tuple-element.297), channel_id=1, source_target_pairs={{4,0},{8,4},{12,8},{16,12},{20,16},{24,20},{28,24},{5,1},{9,5},{13... | collective-permute-start | bytes 6344 | tf_op jit(solution)/shard_map/ppermute | solution.py:25
  424.3 12.4 %collective-permute-start.21 = (f32[1,16,33]{1,0,2:T(1,128)S(1)}, f32[1,16,33]{1,0,2:T(1,128)S(1)}, u32[]{:S(2)}, u32[]{:S(2)}) collective-permute-start(f32[1,16,33]{1,0,2:T(1,128)S(1)} %get-tuple-element.296), channel_id=1, source_target_pairs={{0,4},{4,8},{8,12},{12,16},{16,20},{20,24},{24,28},{1,5},{5,9},{9,... | collective-permute-start | bytes 6344 | tf_op jit(solution)/shard_map/ppermute | solution.py:23
  429.8 6.7 copy-start.9
  436.9 6.2 collective-permute-start.22
  438.2 6.5 collective-permute-start.23
  443.1 1.9 copy-start.40
  514.1 15.2 %collective-permute-start.24 = (f32[1,16,33]{1,0,2:T(1,128)}, f32[1,16,33]{1,0,2:T(1,128)S(1)}, u32[]{:S(2)}, u32[]{:S(2)}) collective-permute-start(f32[1,16,33]{1,0,2:T(1,128)} %get-tuple-element.289), channel_id=1, source_target_pairs={{4,0},{8,4},{12,8},{16,12},{20,16},{24,20},{28,24},{5,1},{9,5},{13... | collective-permute-start | bytes 6344 | tf_op jit(solution)/shard_map/ppermute | solution.py:25
  515.4 13.9 %collective-permute-start.25 = (f32[1,16,33]{1,0,2:T(1,128)}, f32[1,16,33]{1,0,2:T(1,128)S(1)}, u32[]{:S(2)}, u32[]{:S(2)}) collective-permute-start(f32[1,16,33]{1,0,2:T(1,128)} %get-tuple-element.288), channel_id=1, source_target_pairs={{0,4},{4,8},{8,12},{12,16},{16,20},{20,24},{24,28},{1,5},{5,9},{9,... | collective-permute-start | bytes 6344 | tf_op jit(solution)/shard_map/ppermute | solution.py:23
  529.5 6.2 collective-permute-start.26
  530.8 6.5 collective-permute-start.27
  535.7 1.9 copy-start.37
  535.7 1.9 copy-start.38
  595.8 6.4 copy-start.23
  609.2 9.5 %copy-start.3 = (f32[2,16,32,1]{3,2,1,0:T(8,128)S(1)}, f32[2,16,32,1]{3,2,1,0:T(8,128)}, u32[]{:S(2)}) copy-start(f32[2,16,32,1]{3,2,1,0:T(8,128)} %get-tuple-element.197) | copy-start | bytes 12292
  613.9 16.6 %collective-permute-start.28 = (f32[1,16,33]{1,0,2:T(1,128)}, f32[1,16,33]{1,0,2:T(1,128)S(1)}, u32[]{:S(2)}, u32[]{:S(2)}) collective-permute-start(f32[1,16,33]{1,0,2:T(1,128)} %get-tuple-element.280), channel_id=1, source_target_pairs={{4,0},{8,4},{12,8},{16,12},{20,16},{24,20},{28,24},{5,1},{9,5},{13... | collective-permute-start | bytes 6344 | tf_op jit(solution)/shard_map/ppermute | solution.py:25
  615.2 15.3 %collective-permute-start.29 = (f32[1,16,33]{1,0,2:T(1,128)}, f32[1,16,33]{1,0,2:T(1,128)}, u32[]{:S(2)}, u32[]{:S(2)}) collective-permute-start(f32[1,16,33]{1,0,2:T(1,128)} %get-tuple-element.279), channel_id=1, source_target_pairs={{0,4},{4,8},{8,12},{12,16},{16,20},{20,24},{24,28},{1,5},{5,9},{9,... | collective-permute-start | bytes 6344 | tf_op jit(solution)/shard_map/ppermute | solution.py:23
  618.8 2.1 copy-start.12
  618.8 2.1 copy-start.13
  621.9 7.6 copy-start.8
  631.3 7.2 collective-permute-start.30
  632.6 7.0 collective-permute-start.31
  638.5 2.2 copy-start.28
  638.5 2.2 copy-start.35
  638.5 2.2 copy-start.36
  703.1 7.6 copy-start.19
  718.4 12.0 %copy-start.2 = (f32[2,16,32,1]{3,2,1,0:T(8,128)S(1)}, f32[2,16,32,1]{3,2,1,0:T(8,128)}, u32[]{:S(2)}) copy-start(f32[2,16,32,1]{3,2,1,0:T(8,128)} %get-tuple-element.193) | copy-start | bytes 12292
  725.5 16.0 %collective-permute-start.32 = (f32[1,16,33]{1,0,2:T(1,128)}, f32[1,16,33]{1,0,2:T(1,128)}, u32[]{:S(2)}, u32[]{:S(2)}) collective-permute-start(f32[1,16,33]{1,0,2:T(1,128)} %get-tuple-element.270), channel_id=1, source_target_pairs={{4,0},{8,4},{12,8},{16,12},{20,16},{24,20},{28,24},{5,1},{9,5},{13... | collective-permute-start | bytes 6344 | tf_op jit(solution)/shard_map/ppermute | solution.py:25
  726.8 14.7 %collective-permute-start.33 = (f32[1,16,33]{1,0,2:T(1,128)}, f32[1,16,33]{1,0,2:T(1,128)}, u32[]{:S(2)}, u32[]{:S(2)}) collective-permute-start(f32[1,16,33]{1,0,2:T(1,128)} %get-tuple-element.269), channel_id=1, source_target_pairs={{0,4},{4,8},{8,12},{12,16},{16,20},{20,24},{24,28},{1,5},{5,9},{9,... | collective-permute-start | bytes 6344 | tf_op jit(solution)/shard_map/ppermute | solution.py:23
  730.4 2.1 copy-start.10
  730.4 2.1 copy-start.11
  733.6 7.0 copy-start.7
  742.4 7.7 collective-permute-start.34
  743.7 7.0 collective-permute-start.35
  771.9 43.8 %copy-start.24 = (f32[2,16,32]{1,0,2:T(2,128)S(1)}, f32[2,16,32]{1,0,2:T(2,128)}, u32[]{:S(2)}) copy-start(f32[2,16,32]{1,0,2:T(2,128)} %get-tuple-element.161) | copy-start | bytes 12292
  821.4 2.0 copy-start.5
  834.1 12.7 %copy-start.1 = (f32[2,16,32,1]{3,2,1,0:T(8,128)S(1)}, f32[2,16,32,1]{3,2,1,0:T(8,128)}, u32[]{:S(2)}) copy-start(f32[2,16,32,1]{3,2,1,0:T(8,128)} %get-tuple-element.189) | copy-start | bytes 12292
  841.9 17.0 %collective-permute-start.36 = (f32[1,16,33]{1,0,2:T(1,128)}, f32[1,16,33]{1,0,2:T(1,128)}, u32[]{:S(2)}, u32[]{:S(2)}) collective-permute-start(f32[1,16,33]{1,0,2:T(1,128)} %get-tuple-element.259), channel_id=1, source_target_pairs={{4,0},{8,4},{12,8},{16,12},{20,16},{24,20},{28,24},{5,1},{9,5},{13... | collective-permute-start | bytes 6344 | tf_op jit(solution)/shard_map/ppermute | solution.py:25
  843.1 15.7 %collective-permute-start.37 = (f32[1,16,33]{1,0,2:T(1,128)}, f32[1,16,33]{1,0,2:T(1,128)}, u32[]{:S(2)}, u32[]{:S(2)}) collective-permute-start(f32[1,16,33]{1,0,2:T(1,128)} %get-tuple-element.258), channel_id=1, source_target_pairs={{0,4},{4,8},{8,12},{12,16},{16,20},{20,24},{24,28},{1,5},{5,9},{9,... | collective-permute-start | bytes 6344 | tf_op jit(solution)/shard_map/ppermute | solution.py:23
  856.9 1.9 copy-start.6
  860.3 7.7 collective-permute-start.38
  861.6 7.0 collective-permute-start.39
  872.2 3.7 copy-start.20
  (39 other events, 45.7 us)
where the time goes:
time: 965 us; the launch traced here: 951 us
  blocking collectives  457 us (47%)
  between operations  171 us (18%)
  other arithmetic  118 us (12%)
  starting transfers between devices  104 us (11%)
  local copies, waits for them, and re-layouts  87.2 us (9%)
  waiting for transfers between devices  12.9 us (1%)
    psum x10, blocking collectives, shards(): coeffs, total_square = lax.psum((local_dots, image_square), ('gx', 'gy'))  415 us
    ppermute x20, starting transfers between devices, padded_2(): lax.ppermute(tail, axis, [(i, (i + 1) % count) for i in range(ends)])  78.2 us
    div x18, other arithmetic, shards(): basis.append((rest_conc / height, rest_pots / height))  58.3 us
    psum x1, blocking collectives, shards(): start_norm = jnp.sqrt(lax.psum(local_square, ('gx', 'gy')) + epsilon)  42 us
    ppermute x20, starting transfers between devices, padded_2(): lax.ppermute(head, axis, [((i + 1) % count, i) for i in range(ends)])  25.8 us
  transfers between devices with their start and end apart: 40, of which 10 were waited for; matrix products, arithmetic and copies ran while one was open for 4% of the time, Pallas kernels for 0%

commit v1 on v0

v1 whole, which is shorter than its diff:
```python
import functools

import jax
import jax.numpy as jnp
from jax import lax
from jax.experimental import pallas as pl
from jax.experimental.pallas import tpu as pltpu
from jax.sharding import PartitionSpec as P

ITERS = 10
LANES = 128
CHUNK = 16

node_cond = 1.0
plane_cond = 0.5
collector_cond = 2.0
epsilon = 1e-06
MESH = pl.DeviceIdType.MESH


def cycle(
    sizes,
    conc_ref,
    pots_ref,
    diff_ref,
    exch_ref,
    slope_ref,
    sol_conc_ref,
    sol_pots_ref,
    turned,
    basis,
    image,
    edges,
    halos,
    rows,
    sent_rows,
    edge_send,
    edge_recv,
    row_send,
    row_recv,
):
    nx, ny = sizes
    count = nx * ny
    cx, cy = conc_ref.shape[0], conc_ref.shape[1]
    cells = cx * cy
    nodes = exch_ref.shape[2]
    shells = conc_ref.shape[2] // nodes
    groups = LANES // cells
    subs = nodes // groups
    mx = lax.axis_index("gx")
    my = lax.axis_index("gy")
    me = mx * ny + my

    def peers(act):
        if count <= 32:
            for dx in range(nx - 1, -1, -1):
                for dy in range(ny - 1, -1, -1):
                    if dx or dy:
                        act(lax.rem(mx + dx, nx), lax.rem(my + dy, ny))
        else:

            def one(p, carry):
                other = lax.rem(me + p, count)
                act(lax.div(other, ny), lax.rem(other, ny))
                return carry

            lax.fori_loop(1, count, one, 0)

    barrier = pltpu.get_barrier_semaphore()
    peers(
        lambda px, py: pl.semaphore_signal(
            barrier, inc=1, device_id={"gx": px, "gy": py}, device_id_type=MESH
        )
    )

    def fold_nodes(block):
        flat = block.reshape(cells, block.shape[2])
        return flat.T

    def node_register(flat_t):
        return jnp.concatenate(
            [flat_t[g * subs : (g + 1) * subs, :] for g in range(groups)], axis=1
        )

    diff = node_register(fold_nodes(diff_ref[...]))
    exch = node_register(fold_nodes(exch_ref[...]))
    slope = node_register(fold_nodes(slope_ref[...]))
    pots_t = fold_nodes(pots_ref[...])
    pot = node_register(pots_t)
    vol_row = pots_t[nodes : nodes + 1, :]
    vol = jnp.broadcast_to(jnp.concatenate([vol_row] * groups, axis=1), (subs, LANES))

    span = subs * shells
    for x in range(cx):
        for g in range(groups):
            edge_row = g * cells + x * cy
            turned[edge_row : edge_row + cy, :] = conc_ref[x, :, g * span : (g + 1) * span]
    image_flat = turned[...].T
    turned_t = image_flat.reshape(subs, shells, LANES)
    for s in range(subs):
        basis[0, 1 : shells + 1, s, :] = turned_t[s]

    lane = lax.broadcasted_iota(jnp.int32, (subs, LANES), 1)
    sub = lax.broadcasted_iota(jnp.int32, (subs, LANES), 0)
    group = lane // cells
    cell = lane % cells
    cell_x = cell // cy
    cell_y = cell % cy
    single = ((sub == 0) & (group == 0)).astype(jnp.float32)
    first_sub, last_sub = sub == 0, sub == subs - 1
    first_group, last_group = group == 0, group == groups - 1
    inside_low_x, inside_high_x = cell_x > 0, cell_x < cx - 1
    inside_low_y, inside_high_y = cell_y > 0, cell_y < cy - 1
    zero = jnp.zeros((subs, LANES), jnp.float32)
    has = [mx > 0, mx < nx - 1, my > 0, my < ny - 1]

    def roll(value, shift, axis=1):
        shift = shift % value.shape[axis]
        return pltpu.roll(value, shift, axis) if shift else value

    def inner_plane(p):
        return (
            4.0 * p
            - jnp.where(inside_low_x, roll(p, cy), zero)
            - jnp.where(inside_high_x, roll(p, -cy), zero)
            - jnp.where(inside_low_y, roll(p, 1), zero)
            - jnp.where(inside_high_y, roll(p, -1), zero)
        )

    def edge_sum(slot, member):
        low_x = roll(halos[slot, 0, member], -(cx - 1) * cy)
        high_x = roll(halos[slot, 1, member], (cx - 1) * cy)
        low_y = roll(halos[slot, 2, member], -(cy - 1))
        high_y = roll(halos[slot, 3, member], cy - 1)
        return (
            jnp.where(~inside_low_x & has[0], low_x, zero)
            + jnp.where(~inside_high_x & has[1], high_x, zero)
            + jnp.where(~inside_low_y & has[2], low_y, zero)
            + jnp.where(~inside_high_y & has[3], high_y, zero)
        )

    def node_mirror(p):
        low = roll(p, 1, 0)
        inner = jnp.where(first_sub, jnp.where(first_group, p, roll(low, cells)), low)
        high = roll(p, -1, 0)
        outer = jnp.where(last_sub, jnp.where(last_group, p, roll(high, -cells)), high)
        return 2.0 * p - inner - outer

    def node_mean(value):
        total = jnp.broadcast_to(jnp.sum(value, axis=0, keepdims=True), (subs, LANES))
        shift = cells
        while shift < LANES:
            total = total + roll(total, shift)
            shift *= 2
        return total * (1.0 / nodes)

    def edge_copies(slot):
        copies = []
        targets = [
            (lax.rem(mx + 1, nx), my),
            (lax.rem(mx + nx - 1, nx), my),
            (mx, lax.rem(my + 1, ny)),
            (mx, lax.rem(my + ny - 1, ny)),
        ]
        for k, (px, py) in enumerate(targets):
            copies.append(
                pltpu.make_async_remote_copy(
                    src_ref=edges.at[slot],
                    dst_ref=halos.at[slot, k],
                    send_sem=edge_send.at[slot, k],
                    recv_sem=edge_recv.at[slot, k],
                    device_id={"gx": px, "gy": py},
                    device_id_type=MESH,
                )
            )
        return copies

    def pots_image(p, v, ep, ev, surface):
        current = exch * (p - v)
        new_p = (
            node_cond * node_mirror(p)
            + current
            - slope * surface
            + plane_cond * (inner_plane(p) - ep)
        )
        new_v = collector_cond * (inner_plane(v) - ev) - node_mean(current)
        return new_p, new_v, current

    def image_and_dots(step, current, starts):
        def part(at, carry, last):
            here = basis[step, pl.ds(at + 1, CHUNK)]
            low = basis[step, pl.ds(at, CHUNK)]
            high = basis[step, pl.ds(at + 2, CHUNK)]
            new = here + diff[None] * (2.0 * here - low - high)
            if last:
                new = jnp.concatenate([new[:-1], new[-1:] + current[None]], axis=0)
            image[pl.ds(at, CHUNK)] = new
            out = []
            for i in range(step + 1):
                other = here if i == step else basis[i, pl.ds(at + 1, CHUNK)]
                out.append(carry[i] + jnp.sum(other * new, axis=0))
            out.append(carry[step + 1] + jnp.sum(new * new, axis=0))
            if step == 0:
                out.append(carry[2] + jnp.sum(here * here, axis=0))
            return tuple(out)

        parts = shells // CHUNK
        carry = lax.fori_loop(
            0, parts - 1, lambda c, carry: part(c * CHUNK, carry, False), tuple(starts)
        )
        return part((parts - 1) * CHUNK, carry, True)

    def row_copy(step, px, py):
        return pltpu.make_async_remote_copy(
            src_ref=sent_rows.at[step],
            dst_ref=rows.at[step, me],
            send_sem=row_send.at[step],
            recv_sem=row_recv.at[step],
            device_id={"gx": px, "gy": py},
            device_id_type=MESH,
        )

    def send_dots(step, dots):
        padded = -(-len(dots) // 8) * 8
        stacked = [jnp.sum(d, axis=0, keepdims=True) for d in dots]
        stacked += [zero[:1]] * (padded - len(dots))
        tall = jnp.sum(jnp.concatenate(stacked, axis=0), axis=1, keepdims=True)
        at_row = lax.broadcasted_iota(jnp.int32, (padded, LANES), 0)
        at_lane = lax.broadcasted_iota(jnp.int32, (padded, LANES), 1)
        row = jnp.sum(jnp.where(at_row == at_lane, tall, 0.0), axis=0, keepdims=True)
        sent_rows[step] = row
        rows[step, me] = row
        peers(lambda px, py: row_copy(step, px, py).start())

    def wait_rows(step):
        part = rows.at[step, pl.ds(0, count - 1)]
        pltpu.make_async_copy(part, part, row_recv.at[step]).wait()

    def take_dots(step, wanted):
        total = jnp.sum(rows[step], axis=0)
        return [jnp.broadcast_to(total[:, k : k + 1], (subs, LANES)) for k in range(wanted)]

    def pad_ends(step):
        basis[step, 0] = basis[step, 1]
        basis[step, shells + 1] = basis[step, shells]

    pad_ends(0)
    edges[0, 0] = pot
    edges[0, 1] = vol
    pl.semaphore_wait(barrier, count - 1)
    started = edge_copies(0)
    for copy in started:
        copy.start()
    pending = list(started)

    for copy in started:
        copy.wait_recv()
    vecs = [(pot, vol, edge_sum(0, 0), edge_sum(0, 1))]
    cosines, sines, uppers, target = [], [], [], []
    heights = None
    for step in range(ITERS):
        p, v, ep, ev = vecs[step]
        new_p, new_v, current = pots_image(p, v, ep, ev, basis[step, shells])
        more = step < ITERS - 1
        if more:
            edges[step + 1, 0] = new_p
            edges[step + 1, 1] = new_v
            started = edge_copies(step + 1)
            for copy in started:
                copy.start()
            pending += started
        if step > 0:
            pad_ends(step)
        new_v_once = new_v * single
        starts = [vecs[i][0] * new_p + vecs[i][1] * new_v_once for i in range(step + 1)]
        starts.append(new_p * new_p + new_v * new_v_once)
        if step == 0:
            starts.append(pot * pot + vol * (vol * single))
        dots = image_and_dots(step, current, starts)
        send_dots(step, dots)
        wait_rows(step)
        sums = take_dots(step, len(dots))
        scale = None
        if step == 0:
            beta = jnp.sqrt(sums[2] + epsilon)
            scale = 1.0 / beta
            coeffs = [sums[0] * scale * scale]
            square = sums[1] * scale * scale
            target.append(beta)
        else:
            coeffs = list(sums[: step + 1])
            square = sums[step + 1]
        rest = square
        taken = coeffs[0] * coeffs[0]
        for h in coeffs[1:]:
            taken = taken + h * h
        height = jnp.sqrt(square - taken + epsilon)
        inverse = 1.0 / height
        if more:
            for copy in started:
                copy.wait_recv()
            if step == 0:
                vecs[0] = tuple(m * scale for m in vecs[0])
            new = [new_p, new_v, edge_sum(step + 1, 0), edge_sum(step + 1, 1)]
            for k in range(4):
                u = new[k] if step else new[k] * scale
                for i in range(step + 1):
                    u = u - coeffs[i] * vecs[i][k]
                new[k] = u * inverse
            vecs.append(tuple(new))

            def advance(c, carry):
                at = c * CHUNK
                u = image[pl.ds(at, CHUNK)]
                if step == 0:
                    first = basis[0, pl.ds(at + 1, CHUNK)] * scale[None]
                    basis[0, pl.ds(at + 1, CHUNK)] = first
                    u = u * scale[None] - coeffs[0][None] * first
                else:
                    for i in range(step + 1):
                        u = u - coeffs[i][None] * basis[i, pl.ds(at + 1, CHUNK)]
                basis[step + 1, pl.ds(at + 1, CHUNK)] = u * inverse[None]
                return carry

            lax.fori_loop(0, shells // CHUNK, advance, 0)
        entries = coeffs + [height]
        for row in range(step):
            first = cosines[row] * entries[row] + sines[row] * entries[row + 1]
            second = cosines[row] * entries[row + 1] - sines[row] * entries[row]
            entries[row] = first
            entries[row + 1] = second
        radius = jnp.sqrt(entries[step] * entries[step] + entries[step + 1] * entries[step + 1])
        cosine = entries[step] / radius
        sine = entries[step + 1] / radius
        entries[step] = radius
        cosines.append(cosine)
        sines.append(sine)
        lead = target[step]
        target[step] = cosine * lead
        target.append(-sine * lead)
        uppers.append(entries[: step + 1])

    weights = [None] * ITERS
    for row in range(ITERS - 1, -1, -1):
        total = target[row]
        for later in range(row + 1, ITERS):
            total = total - uppers[later][row] * weights[later]
        weights[row] = total / uppers[row][row]

    sol_p = weights[0] * vecs[0][0]
    sol_v = weights[0] * vecs[0][1]
    for i in range(1, ITERS):
        sol_p = sol_p + weights[i] * vecs[i][0]
        sol_v = sol_v + weights[i] * vecs[i][1]

    def combine(c, carry):
        at = c * CHUNK
        total = weights[0][None] * basis[0, pl.ds(at + 1, CHUNK)]
        for i in range(1, ITERS):
            total = total + weights[i][None] * basis[i, pl.ds(at + 1, CHUNK)]
        image[pl.ds(at, CHUNK)] = total
        return carry

    lax.fori_loop(0, shells // CHUNK, combine, 0)
    flat = jnp.concatenate([image[:, s, :] for s in range(subs)], axis=0)
    turned[...] = flat.T
    for x in range(cx):
        for g in range(groups):
            edge_row = g * cells + x * cy
            sol_conc_ref[x, :, g * span : (g + 1) * span] = turned[edge_row : edge_row + cy, :]
    flat_p = jnp.concatenate(
        [sol_p[:, g * cells : (g + 1) * cells] for g in range(groups)] + [sol_v[:1, :cells]], axis=0
    )
    sol_pots_ref[...] = flat_p.T.reshape(cx, cy, nodes + 1)

    for copy in pending:
        copy.wait_send()
    for step in range(ITERS):
        part = rows.at[step, pl.ds(0, count - 1)]
        pltpu.make_async_copy(part, part, row_send.at[step]).wait()


def solution(mesh):
    sizes = (mesh.shape["gx"], mesh.shape["gy"])
    count = sizes[0] * sizes[1]

    def shards(rhs_conc, rhs_pots, diffusion, exchange, slope):
        cells = rhs_conc.shape[0] * rhs_conc.shape[1]
        nodes = exchange.shape[2]
        shells = rhs_conc.shape[2] // nodes
        groups = LANES // cells
        subs = nodes // groups
        vmem = pl.BlockSpec(memory_space=pltpu.VMEM)
        return pl.pallas_call(
            functools.partial(cycle, sizes),
            out_shape=(
                jax.ShapeDtypeStruct(rhs_conc.shape, jnp.float32),
                jax.ShapeDtypeStruct(rhs_pots.shape, jnp.float32),
            ),
            in_specs=[vmem] * 5,
            out_specs=(vmem, vmem),
            scratch_shapes=[
                pltpu.VMEM((LANES, subs * shells), jnp.float32),
                pltpu.VMEM((ITERS, shells + 2, subs, LANES), jnp.float32),
                pltpu.VMEM((shells, subs, LANES), jnp.float32),
                pltpu.VMEM((ITERS, 2, subs, LANES), jnp.float32),
                pltpu.VMEM((ITERS, 4, 2, subs, LANES), jnp.float32),
                pltpu.VMEM((ITERS, count, 1, LANES), jnp.float32),
                pltpu.VMEM((ITERS, 1, LANES), jnp.float32),
                pltpu.SemaphoreType.DMA((ITERS, 4)),
                pltpu.SemaphoreType.DMA((ITERS, 4)),
                pltpu.SemaphoreType.DMA((ITERS,)),
                pltpu.SemaphoreType.DMA((ITERS,)),
            ],
            compiler_params=pltpu.CompilerParams(collective_id=0, has_side_effects=True),
        )(rhs_conc, rhs_pots, diffusion, exchange, slope)

    spec = P("gx", "gy", None)
    return jax.shard_map(
        shards,
        mesh=mesh,
        in_specs=(spec,) * 5,
        out_specs=(spec, spec),
        check_vma=False,
    )
```

time: 965 us -> 67.5 us (0.07); the launches traced: 951 us -> 67.3 us
  blocking collectives: 457 us -> 0 us
  between operations: 171 us -> 0.65 us
  other arithmetic: 118 us -> 0 us
  starting transfers between devices: 104 us -> 0 us
  local copies, waits for them, and re-layouts: 87.2 us -> 2.28 us
  Pallas kernels: 0 us -> 64.4 us
  waiting for transfers between devices: 12.9 us -> 0 us
    psum x11 -> x0, blocking collectives: 457 us -> none  [the longest x10 415 us: shards(): coeffs, total_square = lax.psum((local_dots, image_square), ('gx', 'gy'))]
    ppermute x40 -> x0, starting transfers between devices: 104 us -> none  [the longest x20 78.2 us: padded_2(): lax.ppermute(tail, axis, [(i, (i + 1) % count) for i in range(ends)])]
    pallas_call x0 -> x1, Pallas kernels: none -> 64.4 us  [shards(): pl.pallas_call(functools.partial(cycle, sizes), out_shape=(jax.ShapeDtype...]
    div x20 -> x0, other arithmetic: 58.3 us -> none  [the longest x18 58.3 us: shards(): basis.append((rest_conc / height, rest_pots / height))]
    reduce_sum x41 -> x0, other arithmetic: 32.6 us -> none  [the longest x9 11.6 us: shards(): jnp.sum(vector[0] * image_conc) + jnp.sum(vector[1] * image_pots)]
    slice x79 -> x0, local copies, waits for them, and re-layouts: 28.8 us -> none  [the longest x20 11.6 us: mirror_laplace(): inner = jnp.concatenate([values[..., :1], values[..., :-1]], axis=-1)]
    concatenate x39 -> x0, other arithmetic: 17.3 us -> none  [the longest x9 9.46 us: mirror_laplace(): outer = jnp.concatenate([values[..., 1:], values[..., -1:]], axis=-1)]
    unnamed x139 -> x4, local copies, waits for them, and re-layouts: 18.5 us -> 2.28 us
  transfers between devices with their start and end apart: 40 -> 0, of which waited for: 10 -> 0; matrix products, arithmetic and copies ran while one was open for 4% -> 0% of each run, Pallas kernels for 0% -> 0%
where the time goes in v1:
time: 67.5 us; the launch traced here: 67.3 us
  Pallas kernels  64.4 us (95%)
  local copies, waits for them, and re-layouts  2.28 us (3%)
    pallas_call x1, Pallas kernels, shards(): pl.pallas_call(functools.partial(cycle, sizes), out_shape=(jax.ShapeDtype...  64.4 us
    unnamed x4, local copies, waits for them, and re-layouts  2.28 us

profile of v1, /device:TPU:0, one launch (start us, length us, event | category | flops | bytes accessed | tf_op | source)
XLA Modules:
  0.0 67.3 jit_solution(6396385692822510521)
XLA Ops:
  0.6 64.4 %shard_map.68 = (f32[2,16,2048]{2,1,0:T(8,128)}, f32[2,16,33]{2,1,0:T(8,128)}) custom-call(f32[2,16,2048]{2,1,0:T(8,128)} %conc_ref.1, f32[2,16,33]{2,1,0:T(8,128)} %pots_ref.1, f32[2,16,32]{2,1,0:T(8,128)} %diff_ref.1, f32[2,16,32]{2,1,0:T(8,128)} %exch_ref.1, f32[2,16,32]{2,1,0:T(8,128)} %slope_ref.1), custom_call_target="tpu_custom_call" | custom-call | tf_op jit(solution)/shard_map/pallas_call | solution.py:394
  65.0 0.0 copy-start
  65.0 1.7 %copy.9 = f32[2,16,2048]{2,1,0:T(8,128)} copy(f32[2,16,2048]{2,1,0:T(8,128)} %get-tuple-element.4) | data formatting | bytes 524288
  66.7 0.0 copy-done
  66.7 0.6 copy.10
Async XLA Ops:
  65.0 1.7 %copy-start = (f32[2,16,33]{2,1,0:T(8,128)S(1)}, f32[2,16,33]{2,1,0:T(8,128)}, u32[]{:S(2)}) copy-start(f32[2,16,33]{2,1,0:T(8,128)} %get-tuple-element.5) | copy-start | bytes 12676

commit v2 on v1

--- a/solution.py
+++ b/solution.py
@@ -15,7 +15,77 @@
 plane_cond = 0.5
 collector_cond = 2.0
 epsilon = 1e-06
+first_shift = 3.0
 MESH = pl.DeviceIdType.MESH
+
+
+def add(terms):
+    terms = [t for t in terms if t is not None]
+    while len(terms) > 1:
+        pairs = [terms[k] + terms[k + 1] for k in range(0, len(terms) - 1, 2)]
+        terms = pairs + ([terms[-1]] if len(terms) % 2 else [])
+    return terms[0]
+
+
+def two_columns(last, upper, gram, along1, along2, z11, z12, z22, shift, root, ramp):
+    span = range(last + 1)
+
+    def images_of_rest(cu):
+        out = []
+        for k in span:
+            terms = [cu[i] * upper[i][k] for i in range(max(k - 1, 0), last)]
+            if k == last:
+                terms.append(cu[last] * shift)
+            out.append(add(terms))
+        return out
+
+    h = [along1[i] + shift * gram[i][last] for i in span]
+    cu = [-h[i] for i in span]
+    cu[last] = shift - h[last]
+    gu = [h[i] - add([h[k] * gram[i][k] for k in span]) for i in span]
+    g1 = z11 + shift * along1[last] - add([h[k] * along1[k] for k in span])
+    g2 = z12 + shift * along2[last] - add([h[k] * along2[k] for k in span])
+    square = add([cu[i] * gu[i] for i in span] + [g1])
+    height, inverse = root(ramp(square))
+    col1 = h + [height]
+    first = [c * inverse for c in cu]
+    near = [g * inverse for g in gu]
+    near1, near2 = g1 * inverse, g2 * inverse
+    near_self = ramp(square) * inverse * inverse
+
+    cw = [c * inverse for c in images_of_rest(cu)]
+    c1 = (cu[last] + shift) * inverse
+    c2 = inverse
+    g = [
+        add([cw[k] * gram[i][k] for k in span] + [c1 * along1[i], c2 * along2[i]]) for i in span
+    ]
+    g1 = add([cw[k] * along1[k] for k in span] + [c1 * z11, c2 * z12])
+    g2 = add([cw[k] * along2[k] for k in span] + [c1 * z12, c2 * z22])
+    h = list(g)
+    top = add([first[i] * g[i] for i in span] + [inverse * g1])
+    cu = [cw[i] - h[i] - top * first[i] for i in span]
+    c1 = c1 - top * inverse
+    gu = [g[i] - add([h[k] * gram[i][k] for k in span] + [top * near[i]]) for i in span]
+    g1 = g1 - add([h[k] * along1[k] for k in span] + [top * near1])
+    g2 = g2 - add([h[k] * along2[k] for k in span] + [top * near2])
+    square = add([cu[i] * gu[i] for i in span] + [c1 * g1, c2 * g2])
+    height, inverse2 = root(ramp(square))
+    col2 = h + [top, height]
+    second = ([c * inverse2 for c in cu], c1 * inverse2, c2 * inverse2)
+
+    def next_image(new_shift):
+        cq, d1, d2 = second
+        out = images_of_rest(cq)
+        out = [out[k] - new_shift * cq[k] for k in span]
+        e1 = cq[last] + d1 * (shift - new_shift)
+        e2 = d1 + d2 * (shift - new_shift)
+        return out, e1, e2, d2
+
+    gram = [list(gram[i]) + [near[i], gu[i] * inverse2] for i in span]
+    cross = add([first[i] * gu[i] for i in span] + [inverse * g1]) * inverse2
+    gram.append([gram[i][last + 1] for i in span] + [near_self, cross])
+    gram.append([gram[i][last + 2] for i in span] + [cross, ramp(square) * inverse2 * inverse2])
+    return col1, col2, (first, inverse), second, next_image, gram
 
 
 def cycle(
@@ -29,7 +99,7 @@
     sol_pots_ref,
     turned,
     basis,
-    image,
+    images,
     edges,
     halos,
     rows,
@@ -95,10 +165,9 @@
         for g in range(groups):
             edge_row = g * cells + x * cy
             turned[edge_row : edge_row + cy, :] = conc_ref[x, :, g * span : (g + 1) * span]
-    image_flat = turned[...].T
-    turned_t = image_flat.reshape(subs, shells, LANES)
+    turned_t = turned[...].T.reshape(subs, shells, LANES)
     for s in range(subs):
-        basis[0, 1 : shells + 1, s, :] = turned_t[s]
+        images[2, 1 : shells + 1, s, :] = turned_t[s]
 
     lane = lax.broadcasted_iota(jnp.int32, (subs, LANES), 1)
     sub = lax.broadcasted_iota(jnp.int32, (subs, LANES), 0)
@@ -175,7 +244,8 @@
             )
         return copies
 
-    def pots_image(p, v, ep, ev, surface):
+    def pots_image(vec, surface, shift):
+        p, v, ep, ev = vec
         current = exch * (p - v)
         new_p = (
             node_cond * node_mirror(p)
@@ -184,25 +254,22 @@
             + plane_cond * (inner_plane(p) - ep)
         )
         new_v = collector_cond * (inner_plane(v) - ev) - node_mean(current)
-        return new_p, new_v, current
-
-    def image_and_dots(step, current, starts):
+        return new_p - shift * p, new_v - shift * v, current
+
+    def shells_image(source, target, current, shift, dots=None, starts=()):
+        images[source, 0] = images[source, 1]
+        images[source, shells + 1] = images[source, shells]
+        keep = (1.0 - shift)[None]
+
         def part(at, carry, last):
-            here = basis[step, pl.ds(at + 1, CHUNK)]
-            low = basis[step, pl.ds(at, CHUNK)]
-            high = basis[step, pl.ds(at + 2, CHUNK)]
-            new = here + diff[None] * (2.0 * here - low - high)
+            here = images[source, pl.ds(at + 1, CHUNK)]
+            low = images[source, pl.ds(at, CHUNK)]
+            high = images[source, pl.ds(at + 2, CHUNK)]
+            new = keep * here + diff[None] * (2.0 * here - low - high)
             if last:
                 new = jnp.concatenate([new[:-1], new[-1:] + current[None]], axis=0)
-            image[pl.ds(at, CHUNK)] = new
-            out = []
-            for i in range(step + 1):
-                other = here if i == step else basis[i, pl.ds(at + 1, CHUNK)]
-                out.append(carry[i] + jnp.sum(other * new, axis=0))
-            out.append(carry[step + 1] + jnp.sum(new * new, axis=0))
-            if step == 0:
-                out.append(carry[2] + jnp.sum(here * here, axis=0))
-            return tuple(out)
+            images[target, pl.ds(at + 1, CHUNK)] = new
+            return tuple(dots(at, here, new, carry)) if dots else carry
 
         parts = shells // CHUNK
         carry = lax.fori_loop(
@@ -240,105 +307,164 @@
         total = jnp.sum(rows[step], axis=0)
         return [jnp.broadcast_to(total[:, k : k + 1], (subs, LANES)) for k in range(wanted)]
 
-    def pad_ends(step):
-        basis[step, 0] = basis[step, 1]
-        basis[step, shells + 1] = basis[step, shells]
-
-    pad_ends(0)
-    edges[0, 0] = pot
-    edges[0, 1] = vol
+    pending = []
+
+    def send_edges(slot, p, v):
+        edges[slot, 0] = p
+        edges[slot, 1] = v
+        copies = edge_copies(slot)
+        for copy in copies:
+            copy.start()
+        pending.extend(copies)
+        return copies
+
+    def take_edges(slot, copies, p, v):
+        for copy in copies:
+            copy.wait_recv()
+        return p, v, edge_sum(slot, 0), edge_sum(slot, 1)
+
+    def root(square):
+        height = jnp.sqrt(square + epsilon)
+        return height, 1.0 / height
+
+    def ramp(square):
+        return jnp.maximum(square, 0.0)
+
+    def combine(coeffs, members):
+        return add([c * m for c, m in zip(coeffs, members)])
+
+    columns, cosines, sines, uppers, target = [], [], [], [], []
+
+    def rotate():
+        for step in range(len(uppers), len(columns)):
+            entries = list(columns[step])
+            for row in range(step):
+                first = cosines[row] * entries[row] + sines[row] * entries[row + 1]
+                second = cosines[row] * entries[row + 1] - sines[row] * entries[row]
+                entries[row] = first
+                entries[row + 1] = second
+            square = entries[step] * entries[step] + entries[step + 1] * entries[step + 1]
+            radius = jnp.sqrt(square)
+            cosine = entries[step] / radius
+            sine = entries[step + 1] / radius
+            entries[step] = radius
+            cosines.append(cosine)
+            sines.append(sine)
+            lead = target[step]
+            target[step] = cosine * lead
+            target.append(-sine * lead)
+            uppers.append(entries[: step + 1])
+
+    shift = jnp.full((subs, LANES), first_shift, jnp.float32)
+    images_pots = [None, None, None]
     pl.semaphore_wait(barrier, count - 1)
-    started = edge_copies(0)
-    for copy in started:
-        copy.start()
-    pending = list(started)
-
-    for copy in started:
-        copy.wait_recv()
-    vecs = [(pot, vol, edge_sum(0, 0), edge_sum(0, 1))]
-    cosines, sines, uppers, target = [], [], [], []
-    heights = None
-    for step in range(ITERS):
-        p, v, ep, ev = vecs[step]
-        new_p, new_v, current = pots_image(p, v, ep, ev, basis[step, shells])
-        more = step < ITERS - 1
+    copies = send_edges(0, pot, vol)
+    vecs = [take_edges(0, copies, pot, vol)]
+    p, v, current = pots_image(vecs[0], images[2, shells], shift)
+    copies = send_edges(1, p, v)
+
+    def keep_first(at, here, new, carry):
+        basis[0, pl.ds(at, CHUNK)] = here
+        return carry
+
+    shells_image(2, 0, current, shift, keep_first)
+    images_pots[0] = take_edges(1, copies, p, v)
+    p, v, current = pots_image(images_pots[0], images[0, shells], shift)
+    slot = 2
+    copies = send_edges(slot, p, v)
+    gram = None
+    for last in range(0, ITERS, 2):
+        block = last // 2
+        more = last + 2 < ITERS
+        v_once = v * single
+        z1 = images_pots[0]
+        z1_once = z1[1] * single
+        starts = [vecs[i][0] * z1[0] + vecs[i][1] * z1_once for i in range(last + 1)]
+        starts += [vecs[i][0] * p + vecs[i][1] * v_once for i in range(last + 1)]
+        starts += [z1[0] * z1[0] + z1[1] * z1_once]
+        starts += [z1[0] * p + z1[1] * v_once, p * p + v * v_once]
+        if block == 0:
+            starts.append(pot * pot + vol * (vol * single))
+
+        def dots(at, here, new, carry):
+            others = [basis[i, pl.ds(at, CHUNK)] for i in range(last + 1)]
+            out = [jnp.sum(q * here, axis=0) for q in others]
+            out += [jnp.sum(q * new, axis=0) for q in others]
+            out += [jnp.sum(m * n, axis=0) for m, n in ((here, here), (here, new), (new, new))]
+            if block == 0:
+                out.append(jnp.sum(others[0] * others[0], axis=0))
+            return [c + o for c, o in zip(carry, out)]
+
+        products = shells_image(0, 1, current, shift, dots, starts)
+        send_dots(block, products)
+        rotate()
         if more:
-            edges[step + 1, 0] = new_p
-            edges[step + 1, 1] = new_v
-            started = edge_copies(step + 1)
-            for copy in started:
-                copy.start()
-            pending += started
-        if step > 0:
-            pad_ends(step)
-        new_v_once = new_v * single
-        starts = [vecs[i][0] * new_p + vecs[i][1] * new_v_once for i in range(step + 1)]
-        starts.append(new_p * new_p + new_v * new_v_once)
-        if step == 0:
-            starts.append(pot * pot + vol * (vol * single))
-        dots = image_and_dots(step, current, starts)
-        send_dots(step, dots)
-        wait_rows(step)
-        sums = take_dots(step, len(dots))
+            images_pots[1] = take_edges(slot, copies, p, v)
+            p, v, current = pots_image(images_pots[1], images[1, shells], shift)
+            slot += 1
+            copies = send_edges(slot, p, v)
+            shells_image(1, 2, current, shift)
+        wait_rows(block)
+        sums = take_dots(block, len(products))
         scale = None
-        if step == 0:
-            beta = jnp.sqrt(sums[2] + epsilon)
-            scale = 1.0 / beta
-            coeffs = [sums[0] * scale * scale]
-            square = sums[1] * scale * scale
+        if block == 0:
+            beta, scale = root(sums[5])
             target.append(beta)
-        else:
-            coeffs = list(sums[: step + 1])
-            square = sums[step + 1]
-        rest = square
-        taken = coeffs[0] * coeffs[0]
-        for h in coeffs[1:]:
-            taken = taken + h * h
-        height = jnp.sqrt(square - taken + epsilon)
-        inverse = 1.0 / height
-        if more:
-            for copy in started:
-                copy.wait_recv()
-            if step == 0:
-                vecs[0] = tuple(m * scale for m in vecs[0])
-            new = [new_p, new_v, edge_sum(step + 1, 0), edge_sum(step + 1, 1)]
-            for k in range(4):
-                u = new[k] if step else new[k] * scale
-                for i in range(step + 1):
-                    u = u - coeffs[i] * vecs[i][k]
-                new[k] = u * inverse
-            vecs.append(tuple(new))
-
-            def advance(c, carry):
-                at = c * CHUNK
-                u = image[pl.ds(at, CHUNK)]
-                if step == 0:
-                    first = basis[0, pl.ds(at + 1, CHUNK)] * scale[None]
-                    basis[0, pl.ds(at + 1, CHUNK)] = first
-                    u = u * scale[None] - coeffs[0][None] * first
-                else:
-                    for i in range(step + 1):
-                        u = u - coeffs[i][None] * basis[i, pl.ds(at + 1, CHUNK)]
-                basis[step + 1, pl.ds(at + 1, CHUNK)] = u * inverse[None]
-                return carry
-
-            lax.fori_loop(0, shells // CHUNK, advance, 0)
-        entries = coeffs + [height]
-        for row in range(step):
-            first = cosines[row] * entries[row] + sines[row] * entries[row + 1]
-            second = cosines[row] * entries[row + 1] - sines[row] * entries[row]
-            entries[row] = first
-            entries[row + 1] = second
-        radius = jnp.sqrt(entries[step] * entries[step] + entries[step + 1] * entries[step + 1])
-        cosine = entries[step] / radius
-        sine = entries[step + 1] / radius
-        entries[step] = radius
-        cosines.append(cosine)
-        sines.append(sine)
-        lead = target[step]
-        target[step] = cosine * lead
-        target.append(-sine * lead)
-        uppers.append(entries[: step + 1])
+            sums = [s * scale * scale for s in sums]
+            gram = [[sums[5]]]
+        width = last + 1
+        col1, col2, first, second, next_image, gram = two_columns(
+            last,
+            columns,
+            gram,
+            sums[:width],
+            sums[width : 2 * width],
+            sums[2 * width],
+            sums[2 * width + 1],
+            sums[2 * width + 2],
+            shift,
+            root,
+            ramp,
+        )
+        columns += [col1, col2]
+        if not more:
+            break
+        new_shift = col1[last]
+        along, e1, e2, e3 = next_image(new_shift)
+        one = first[0] + [first[1]]
+        two = second[0] + [second[1], second[2]]
+        three = along + [e1, e2, e3]
+        shift = new_shift
+        if block == 0:
+            one, two, three = ([c * scale for c in cs] for cs in (one, two, three))
+        images_pots[2] = take_edges(slot, copies, p, v)
+        members = [list(m) for m in zip(*(vecs + images_pots))]
+        new_vecs = [tuple(combine(cs, m) for m in members) for cs in (one, two, three)]
+        if block == 0:
+            vecs[0] = tuple(m * scale for m in vecs[0])
+        vecs += new_vecs[:2]
+        images_pots = [new_vecs[2], None, None]
+        surfaces = [basis[i, shells - 1] for i in range(width)] + [
+            images[k, shells] for k in range(3)
+        ]
+        p, v, current = pots_image(images_pots[0], combine(three, surfaces), shift)
+        if last + 4 < ITERS:
+            slot += 1
+            copies = send_edges(slot, p, v)
+
+        def advance(c, carry):
+            at = c * CHUNK
+            parts = [basis[i, pl.ds(at, CHUNK)] for i in range(width)]
+            parts += [images[k, pl.ds(at + 1, CHUNK)] for k in range(3)]
+            basis[last + 1, pl.ds(at, CHUNK)] = combine(one, parts)
+            basis[last + 2, pl.ds(at, CHUNK)] = combine(two, parts)
+            images[0, pl.ds(at + 1, CHUNK)] = combine(three, parts)
+            if block == 0:
+                basis[0, pl.ds(at, CHUNK)] = parts[0] * scale
+            return carry
+
+        lax.fori_loop(0, shells // CHUNK, advance, 0)
+    rotate()
 
     weights = [None] * ITERS
     for row in range(ITERS - 1, -1, -1):
@@ -346,23 +472,21 @@
         for later in range(row + 1, ITERS):
             total = total - uppers[later][row] * weights[later]
         weights[row] = total / uppers[row][row]
-
-    sol_p = weights[0] * vecs[0][0]
-    sol_v = weights[0] * vecs[0][1]
-    for i in range(1, ITERS):
-        sol_p = sol_p + weights[i] * vecs[i][0]
-        sol_v = sol_v + weights[i] * vecs[i][1]
-
-    def combine(c, carry):
+    tail = weights[ITERS - 1]
+    mixed = [weights[i] + tail * first[0][i] for i in range(ITERS - 1)] + [tail * first[1]]
+
+    sol_p = combine(mixed, [m[0] for m in vecs] + [images_pots[0][0]])
+    sol_v = combine(mixed, [m[1] for m in vecs] + [images_pots[0][1]])
+
+    def gather(c, carry):
         at = c * CHUNK
-        total = weights[0][None] * basis[0, pl.ds(at + 1, CHUNK)]
-        for i in range(1, ITERS):
-            total = total + weights[i][None] * basis[i, pl.ds(at + 1, CHUNK)]
-        image[pl.ds(at, CHUNK)] = total
+        parts = [basis[i, pl.ds(at, CHUNK)] for i in range(ITERS - 1)]
+        parts.append(images[0, pl.ds(at + 1, CHUNK)])
+        images[1, pl.ds(at + 1, CHUNK)] = combine(mixed, parts)
         return carry
 
-    lax.fori_loop(0, shells // CHUNK, combine, 0)
-    flat = jnp.concatenate([image[:, s, :] for s in range(subs)], axis=0)
+    lax.fori_loop(0, shells // CHUNK, gather, 0)
+    flat = jnp.concatenate([images[1, 1 : shells + 1, s, :] for s in range(subs)], axis=0)
     turned[...] = flat.T
     for x in range(cx):
         for g in range(groups):
@@ -375,7 +499,7 @@
 
     for copy in pending:
         copy.wait_send()
-    for step in range(ITERS):
+    for step in range(ITERS // 2):
         part = rows.at[step, pl.ds(0, count - 1)]
         pltpu.make_async_copy(part, part, row_send.at[step]).wait()
 
@@ -401,16 +525,16 @@
             out_specs=(vmem, vmem),
             scratch_shapes=[
                 pltpu.VMEM((LANES, subs * shells), jnp.float32),
-                pltpu.VMEM((ITERS, shells + 2, subs, LANES), jnp.float32),
-                pltpu.VMEM((shells, subs, LANES), jnp.float32),
+                pltpu.VMEM((ITERS - 1, shells, subs, LANES), jnp.float32),
+                pltpu.VMEM((3, shells + 2, subs, LANES), jnp.float32),
                 pltpu.VMEM((ITERS, 2, subs, LANES), jnp.float32),
                 pltpu.VMEM((ITERS, 4, 2, subs, LANES), jnp.float32),
-                pltpu.VMEM((ITERS, count, 1, LANES), jnp.float32),
-                pltpu.VMEM((ITERS, 1, LANES), jnp.float32),
+                pltpu.VMEM((ITERS // 2, count, 1, LANES), jnp.float32),
+                pltpu.VMEM((ITERS // 2, 1, LANES), jnp.float32),
                 pltpu.SemaphoreType.DMA((ITERS, 4)),
                 pltpu.SemaphoreType.DMA((ITERS, 4)),
-                pltpu.SemaphoreType.DMA((ITERS,)),
-                pltpu.SemaphoreType.DMA((ITERS,)),
+                pltpu.SemaphoreType.DMA((ITERS // 2,)),
+                pltpu.SemaphoreType.DMA((ITERS // 2,)),
             ],
             compiler_params=pltpu.CompilerParams(collective_id=0, has_side_effects=True),
         )(rhs_conc, rhs_pots, diffusion, exchange, slope)

time: 67.5 us -> 55.1 us (0.82)
  Pallas kernels: 64.4 us -> 52 us
    pallas_call x1, Pallas kernels: 64.4 us -> 52 us  [shards(): pl.pallas_call(functools.partial(cycle, sizes), out_shape=(jax.ShapeDtype...]
where the time goes in v2:
time: 55.1 us; the launch traced here: 54.9 us
  Pallas kernels  52 us (94%)
  local copies, waits for them, and re-layouts  2.28 us (4%)
  between operations  0.65 us (1%)
    pallas_call x1, Pallas kernels, shards(): pl.pallas_call(functools.partial(cycle, sizes), out_shape=(jax.ShapeDtype...  52 us
    unnamed x4, local copies, waits for them, and re-layouts  2.28 us

profile of v2, /device:TPU:0, one launch (start us, length us, event | category | flops | bytes accessed | tf_op | source)
XLA Modules:
  0.0 54.9 jit_solution(12087798647725273544)
XLA Ops:
  0.6 52.0 %shard_map.68 = (f32[2,16,2048]{2,1,0:T(8,128)}, f32[2,16,33]{2,1,0:T(8,128)}) custom-call(f32[2,16,2048]{2,1,0:T(8,128)} %conc_ref.1, f32[2,16,33]{2,1,0:T(8,128)} %pots_ref.1, f32[2,16,32]{2,1,0:T(8,128)} %diff_ref.1, f32[2,16,32]{2,1,0:T(8,128)} %exch_ref.1, f32[2,16,32]{2,1,0:T(8,128)} %slope_ref.1), custom_call_target="tpu_custom_call" | custom-call | tf_op jit(solution)/shard_map/pallas_call | solution.py:518
  52.6 0.0 copy-start
  52.6 1.7 %copy.9 = f32[2,16,2048]{2,1,0:T(8,128)} copy(f32[2,16,2048]{2,1,0:T(8,128)} %get-tuple-element.4) | data formatting | bytes 524288
  54.3 0.0 copy-done
  54.3 0.6 %copy.10 = f32[2,16,33]{2,1,0:T(8,128)} copy(f32[2,16,33]{2,1,0:T(8,128)S(1)} %copy-done) | data formatting | bytes 8448
Async XLA Ops:
  52.6 1.7 %copy-start = (f32[2,16,33]{2,1,0:T(8,128)S(1)}, f32[2,16,33]{2,1,0:T(8,128)}, u32[]{:S(2)}) copy-start(f32[2,16,33]{2,1,0:T(8,128)} %get-tuple-element.5) | copy-start | bytes 12676

commit v3 on v2

--- a/solution.py
+++ b/solution.py
@@ -182,6 +182,7 @@
     inside_low_y, inside_high_y = cell_y > 0, cell_y < cy - 1
     zero = jnp.zeros((subs, LANES), jnp.float32)
     has = [mx > 0, mx < nx - 1, my > 0, my < ny - 1]
+    goes = [has[1], has[0], has[3], has[2]]
 
     def roll(value, shift, axis=1):
         shift = shift % value.shape[axis]
@@ -313,14 +314,14 @@
         edges[slot, 0] = p
         edges[slot, 1] = v
         copies = edge_copies(slot)
-        for copy in copies:
-            copy.start()
-        pending.extend(copies)
+        for copy, there in zip(copies, goes):
+            pl.when(there)(copy.start)
+        pending.append(copies)
         return copies
 
     def take_edges(slot, copies, p, v):
-        for copy in copies:
-            copy.wait_recv()
+        for copy, there in zip(copies, has):
+            pl.when(there)(copy.wait_recv)
         return p, v, edge_sum(slot, 0), edge_sum(slot, 1)
 
     def root(square):
@@ -497,8 +498,9 @@
     )
     sol_pots_ref[...] = flat_p.T.reshape(cx, cy, nodes + 1)
 
-    for copy in pending:
-        copy.wait_send()
+    for copies in pending:
+        for copy, there in zip(copies, goes):
+            pl.when(there)(copy.wait_send)
     for step in range(ITERS // 2):
         part = rows.at[step, pl.ds(0, count - 1)]
         pltpu.make_async_copy(part, part, row_send.at[step]).wait()

time: 55.1 us -> 47.1 us (0.85)
  Pallas kernels: 52 us -> 44 us
    pallas_call x1, Pallas kernels: 52 us -> 44 us  [shards(): pl.pallas_call(functools.partial(cycle, sizes), out_shape=(jax.ShapeDtype...]
where the time goes in v3:
time: 47.1 us; the launch traced here: 47 us
  Pallas kernels  44 us (93%)
  local copies, waits for them, and re-layouts  2.28 us (5%)
  between operations  0.65 us (1%)
    pallas_call x1, Pallas kernels, shards(): pl.pallas_call(functools.partial(cycle, sizes), out_shape=(jax.ShapeDtype...  44 us
    unnamed x4, local copies, waits for them, and re-layouts  2.28 us

profile of v3, /device:TPU:0, one launch (start us, length us, event | category | flops | bytes accessed | tf_op | source)
XLA Modules:
  0.0 47.0 jit_solution(17787331153488357252)
XLA Ops:
  0.6 44.0 %shard_map.68 = (f32[2,16,2048]{2,1,0:T(8,128)}, f32[2,16,33]{2,1,0:T(8,128)}) custom-call(f32[2,16,2048]{2,1,0:T(8,128)} %conc_ref.1, f32[2,16,33]{2,1,0:T(8,128)} %pots_ref.1, f32[2,16,32]{2,1,0:T(8,128)} %diff_ref.1, f32[2,16,32]{2,1,0:T(8,128)} %exch_ref.1, f32[2,16,32]{2,1,0:T(8,128)} %slope_ref.1), custom_call_target="tpu_custom_call" | custom-call | tf_op jit(solution)/shard_map/pallas_call | solution.py:520
  44.7 0.0 copy-start
  44.7 1.7 %copy.9 = f32[2,16,2048]{2,1,0:T(8,128)} copy(f32[2,16,2048]{2,1,0:T(8,128)} %get-tuple-element.4) | data formatting | bytes 524288
  46.3 0.0 copy-done
  46.3 0.6 %copy.10 = f32[2,16,33]{2,1,0:T(8,128)} copy(f32[2,16,33]{2,1,0:T(8,128)S(1)} %copy-done) | data formatting | bytes 8448
Async XLA Ops:
  44.7 1.7 %copy-start = (f32[2,16,33]{2,1,0:T(8,128)S(1)}, f32[2,16,33]{2,1,0:T(8,128)}, u32[]{:S(2)}) copy-start(f32[2,16,33]{2,1,0:T(8,128)} %get-tuple-element.5) | copy-start | bytes 12676

commit v4 on v3

--- a/solution.py
+++ b/solution.py
@@ -108,6 +108,7 @@
     edge_recv,
     row_send,
     row_recv,
+    load_sem,
 ):
     nx, ny = sizes
     count = nx * ny
@@ -143,6 +144,21 @@
         )
     )
 
+    span = subs * shells
+    loads = []
+    for x in range(cx):
+        for g in range(groups):
+            edge_row = g * cells + x * cy
+            loads.append(
+                pltpu.make_async_copy(
+                    conc_ref.at[x, :, g * span : (g + 1) * span],
+                    turned.at[edge_row : edge_row + cy, :],
+                    load_sem.at[x, g],
+                )
+            )
+    for copy in loads:
+        copy.start()
+
     def fold_nodes(block):
         flat = block.reshape(cells, block.shape[2])
         return flat.T
@@ -160,11 +176,8 @@
     vol_row = pots_t[nodes : nodes + 1, :]
     vol = jnp.broadcast_to(jnp.concatenate([vol_row] * groups, axis=1), (subs, LANES))
 
-    span = subs * shells
-    for x in range(cx):
-        for g in range(groups):
-            edge_row = g * cells + x * cy
-            turned[edge_row : edge_row + cy, :] = conc_ref[x, :, g * span : (g + 1) * span]
+    for copy in loads:
+        copy.wait()
     turned_t = turned[...].T.reshape(subs, shells, LANES)
     for s in range(subs):
         images[2, 1 : shells + 1, s, :] = turned_t[s]
@@ -470,9 +483,9 @@
     weights = [None] * ITERS
     for row in range(ITERS - 1, -1, -1):
         total = target[row]
-        for later in range(row + 1, ITERS):
+        for later in range(ITERS - 1, row, -1):
             total = total - uppers[later][row] * weights[later]
-        weights[row] = total / uppers[row][row]
+        weights[row] = total * (1.0 / uppers[row][row])
     tail = weights[ITERS - 1]
     mixed = [weights[i] + tail * first[0][i] for i in range(ITERS - 1)] + [tail * first[1]]
 
@@ -523,7 +536,7 @@
                 jax.ShapeDtypeStruct(rhs_conc.shape, jnp.float32),
                 jax.ShapeDtypeStruct(rhs_pots.shape, jnp.float32),
             ),
-            in_specs=[vmem] * 5,
+            in_specs=[pl.BlockSpec(memory_space=pl.ANY)] + [vmem] * 4,
             out_specs=(vmem, vmem),
             scratch_shapes=[
                 pltpu.VMEM((LANES, subs * shells), jnp.float32),
@@ -537,6 +550,7 @@
                 pltpu.SemaphoreType.DMA((ITERS, 4)),
                 pltpu.SemaphoreType.DMA((ITERS // 2,)),
                 pltpu.SemaphoreType.DMA((ITERS // 2,)),
+                pltpu.SemaphoreType.DMA((rhs_conc.shape[0], groups)),
             ],
             compiler_params=pltpu.CompilerParams(collective_id=0, has_side_effects=True),
         )(rhs_conc, rhs_pots, diffusion, exchange, slope)

time: 47.1 us -> 47.1 us (level)
  no operation moved by 1% of the time
where the time goes in v4:
time: 47.1 us; the launch traced here: 46.7 us
  Pallas kernels  43.8 us (93%)
  local copies, waits for them, and re-layouts  2.28 us (5%)
  between operations  0.65 us (1%)
    pallas_call x1, Pallas kernels, shards(): pl.pallas_call(functools.partial(cycle, sizes), out_shape=(jax.ShapeDtype...  43.8 us
    unnamed x4, local copies, waits for them, and re-layouts  2.28 us

profile of v4, /device:TPU:0, one launch (start us, length us, event | category | flops | bytes accessed | tf_op | source)
XLA Modules:
  0.0 46.7 jit_solution(7032890055204663286)
XLA Ops:
  0.6 43.8 %shard_map.68 = (f32[2,16,2048]{2,1,0:T(8,128)}, f32[2,16,33]{2,1,0:T(8,128)}) custom-call(f32[2,16,2048]{2,1,0:T(8,128)} %conc_ref.1, f32[2,16,33]{2,1,0:T(8,128)} %pots_ref.1, f32[2,16,32]{2,1,0:T(8,128)} %diff_ref.1, f32[2,16,32]{2,1,0:T(8,128)} %exch_ref.1, f32[2,16,32]{2,1,0:T(8,128)} %slope_ref.1), custom_call_target="tpu_custom_call" | custom-call | tf_op jit(solution)/shard_map/pallas_call | solution.py:533
  44.5 0.0 copy-start
  44.5 1.7 %copy.9 = f32[2,16,2048]{2,1,0:T(8,128)} copy(f32[2,16,2048]{2,1,0:T(8,128)} %get-tuple-element.4) | data formatting | bytes 524288
  46.1 0.0 copy-done
  46.1 0.6 %copy.10 = f32[2,16,33]{2,1,0:T(8,128)} copy(f32[2,16,33]{2,1,0:T(8,128)S(1)} %copy-done) | data formatting | bytes 8448
Async XLA Ops:
  44.5 1.7 %copy-start = (f32[2,16,33]{2,1,0:T(8,128)S(1)}, f32[2,16,33]{2,1,0:T(8,128)}, u32[]{:S(2)}) copy-start(f32[2,16,33]{2,1,0:T(8,128)} %get-tuple-element.5) | copy-start | bytes 12676
